TPU v7x, 32 devices: a whole 2x2x4 slice. The times are simulated.
32 devices in a mesh: lat: 8 (over z, x), lon: 4 (over y, core).
Axes of the slice: x: 2, y: 2, z: 4, core: 2. Of those that a mesh axis runs over, the one named last changes fastest.
Arguments:
- courant: float32 [2, 16, 128, 512], P(None, None, 'lat', 'lon'), may hold values from -0.45 to 0.45
- obs_matrix: float32 [8, 32, 128, 128], P('lat', 'lon'), may hold values from -0.5 to 0.5
- obs_weight: float32 [8, 32, 128], P('lat', 'lon'), may hold values from 0.5 to 4
- innovation: float32 [8, 32, 128], P('lat', 'lon'), may hold values from -6 to 6
- block_owner: int32 [8, 32, 1], P('lat', 'lon'), may hold values from 0 to 3; in each aligned block of 8 rows (0 to 7, 8 to 15, ..., all dimensions but the last counted through in order) at most 2 rows name the same one
- block_row: int32 [8, 32], P('lat', 'lon'), may hold values from 0 to 255
- block_count: int32 [8, 4], P('lat', 'lon'), may hold values from 1 to 8, as said below
Outputs:
- increment: float32 [16, 128, 512], P(None, 'lat', 'lon')
- residual: float32 [16, 128, 512], P(None, 'lat', 'lon')
Inputs may be any that keep to these rules, and one draw needn't show every extreme that they name: `block_owner`: among one device's 8 block slots no lon index is named more than 2 times, a bound that some block reaches. A device's first block_count slots are live, the rest are padding; some device has all 8 live.
All inputs are finite; a program needn't handle non-finite values.
Results may differ from a plain program's by a relative error of at most 0.0003.
Values sent between devices are 32-bit elements; how exact they have to be, the bound alone decides.
A program may use at most 64 MiB of HBM per device.

v0:
```python
import jax
import jax.numpy as jnp
from jax import lax
from jax.sharding import PartitionSpec as P

SLOT = 2
STEPS = 4
ITERS = 2


def padded_2(cells, sides, width):
    for axis, dim in sides:
        count = lax.axis_size(axis)
        head = lax.slice_in_dim(cells, 0, width, axis=dim)
        tail = lax.slice_in_dim(cells, cells.shape[dim] - width, cells.shape[dim], axis=dim)
        cells = jnp.concatenate(
            [
                lax.ppermute(tail, axis, [(i, (i + 1) % count) for i in range(count)]),
                cells,
                lax.ppermute(head, axis, [((i + 1) % count, i) for i in range(count)]),
            ],
            axis=dim,
        )
    return cells


def window(array_in, row_start, col_start, row_span, col_span):
    rows_cut = lax.slice_in_dim(array_in, row_start, row_start + row_span, axis=array_in.ndim - 2)
    return lax.slice_in_dim(rows_cut, col_start, col_start + col_span, axis=array_in.ndim - 1)


def shards(courant, obs_matrix, obs_weight, innovation, block_owner, block_row, block_count):
    levels = courant.shape[1]
    lat_rows = courant.shape[2]
    lon_cells = courant.shape[3]
    capacity = block_row.shape[1]
    lon_count = lax.axis_size("lon")
    lat_index = lax.axis_index("lat")
    lat_total = lax.axis_size("lat")
    rate_parts = jnp.stack(
        [
            jnp.maximum(courant[0], 0.0),
            jnp.maximum(-courant[0], 0.0),
            jnp.maximum(courant[1], 0.0),
            jnp.maximum(-courant[1], 0.0),
        ]
    )

    def edge_mask(margin):
        global_rows = (
            jnp.arange(lat_rows + 2 * margin, dtype=jnp.int32) + lat_index * lat_rows - margin
        )
        inside = (global_rows >= 0) & (global_rows < lat_rows * lat_total)
        return jnp.where(inside, 1.0, 0.0).astype(jnp.float32)[:, None]

    deep_rates = padded_2(rate_parts, (("lat", 2), ("lon", 3)), STEPS)
    deep_keep = 1.0 - deep_rates[0] - deep_rates[1] - deep_rates[2] - deep_rates[3]

    def model_adjoint(grid_field):
        padded = padded_2(grid_field, (("lat", 1), ("lon", 2)), STEPS) * edge_mask(STEPS)
        for sweep in range(STEPS):
            margin = STEPS - sweep - 1
            offset = sweep + 1
            row_span = lat_rows + 2 * margin
            col_span = lon_cells + 2 * margin
            fresh_field = (
                window(deep_keep, offset, offset, row_span, col_span) * padded[:, 1:-1, 1:-1]
                + window(deep_rates[0], offset + 1, offset, row_span, col_span)
                * padded[:, 2:, 1:-1]
                + window(deep_rates[1], offset - 1, offset, row_span, col_span)
                * padded[:, :-2, 1:-1]
                + window(deep_rates[2], offset, offset + 1, row_span, col_span)
                * padded[:, 1:-1, 2:]
                + window(deep_rates[3], offset, offset - 1, row_span, col_span)
                * padded[:, 1:-1, :-2]
            )
            padded = fresh_field * edge_mask(margin)
        return padded

    owner_lon = block_owner[0, :, 0]
    onehot = (owner_lon[:, None] == jnp.arange(lon_count, dtype=jnp.int32)[None, :]).astype(
        jnp.int32
    )
    before = jnp.cumsum(onehot, axis=0) - onehot
    target = owner_lon * SLOT + jnp.sum(before * onehot, axis=1)
    live_mask = jnp.arange(capacity, dtype=jnp.int32) < block_count[0, 0]
    weighted = jnp.where(live_mask[:, None], obs_weight[0], 0.0)
    requests = (
        jnp.full((lon_count * SLOT,), -1, jnp.int32)
        .at[target]
        .set(jnp.where(live_mask, block_row[0], -1))
    )
    asked_raw = lax.all_to_all(requests, "lon", split_axis=0, concat_axis=0, tiled=True)
    asked_rows = jnp.maximum(asked_raw, 0)

    def accumulate(block_terms):
        flat_out = (
            jnp.zeros((levels * lat_rows, lon_cells), jnp.float32).at[asked_rows].add(block_terms)
        )
        return flat_out.reshape(levels, lat_rows, lon_cells)

    def to_owner(block_terms):
        outgoing = jnp.zeros((lon_count * SLOT, lon_cells), jnp.float32).at[target].set(block_terms)
        return accumulate(lax.all_to_all(outgoing, "lon", split_axis=0, concat_axis=0, tiled=True))

    departure = to_owner(
        jnp.einsum(
            "bok,bo->bk", obs_matrix[0], weighted * innovation[0], precision=lax.Precision.HIGHEST
        )
    )
    right_side = model_adjoint(departure)
    increment = jnp.zeros_like(right_side)
    residual = right_side

    def squares(vector):
        return lax.psum(jnp.sum(vector * vector), ("lat", "lon"))

    direction = right_side
    norm_now = squares(residual)
    for sweep in range(ITERS):
        model_padded = padded_2(direction, (("lat", 1), ("lon", 2)), STEPS) * edge_mask(STEPS)
        for model_sweep in range(STEPS):
            model_margin = STEPS - model_sweep - 1
            model_offset = model_sweep + 1
            model_row_span = lat_rows + 2 * model_margin
            model_col_span = lon_cells + 2 * model_margin
            model_fresh_field = (
                window(deep_keep, model_offset, model_offset, model_row_span, model_col_span)
                * model_padded[:, 1:-1, 1:-1]
                + window(deep_rates[0], model_offset, model_offset, model_row_span, model_col_span)
                * model_padded[:, :-2, 1:-1]
                + window(deep_rates[1], model_offset, model_offset, model_row_span, model_col_span)
                * model_padded[:, 2:, 1:-1]
                + window(deep_rates[2], model_offset, model_offset, model_row_span, model_col_span)
                * model_padded[:, 1:-1, :-2]
                + window(deep_rates[3], model_offset, model_offset, model_row_span, model_col_span)
                * model_padded[:, 1:-1, 2:]
            )
            model_padded = model_fresh_field * edge_mask(model_margin)
        state_rows = model_padded.reshape(levels * lat_rows, lon_cells)
        fetched = lax.all_to_all(
            state_rows[asked_rows], "lon", split_axis=0, concat_axis=0, tiled=True
        )
        seen_rows = fetched[target]
        predicted = jnp.einsum(
            "bok,bk->bo", obs_matrix[0], seen_rows, precision=lax.Precision.HIGHEST
        )
        image_vec = direction + model_adjoint(
            to_owner(
                jnp.einsum(
                    "bok,bo->bk",
                    obs_matrix[0],
                    weighted * predicted,
                    precision=lax.Precision.HIGHEST,
                )
            )
        )
        step_size = norm_now / lax.psum(jnp.sum(direction * image_vec), ("lat", "lon"))
        increment = increment + step_size * direction
        residual = residual - step_size * image_vec
        if sweep + 1 < ITERS:
            norm_next = squares(residual)
            direction = residual + norm_next / norm_now * direction
            norm_now = norm_next
    return (increment, residual)


def solution(mesh):
    placed = (
        P(None, None, "lat", "lon"),
        P("lat", "lon", None, None),
        P("lat", "lon", None),
        P("lat", "lon", None),
        P("lat", "lon", None),
        P("lat", "lon"),
        P("lat", "lon"),
    )
    return jax.shard_map(
        shards,
        mesh=mesh,
        in_specs=placed,
        out_specs=(P(None, "lat", "lon"), P(None, "lat", "lon")),
        check_vma=False,
    )
```

profile of v0, /device:TPU:0, one launch (start us, length us, event | category | flops | bytes accessed | tf_op | source)
XLA Modules:
  0.0 282.4 jit_solution(7485044574819764347)
XLA Ops:
  0.7 1.1 slice_maximum_fusion.1
  1.8 3.0 %collective-permute-start = (f32[4,16,4,128]{3,2,1,0:T(4,128)S(1)}, f32[4,16,4,128]{3,2,1,0:T(4,128)S(1)}, u32[]{:S(2)}, u32[]{:S(2)}) collective-permute-start(f32[4,16,4,128]{3,2,1,0:T(4,128)S(1)} %get-tuple-element.17), channel_id=1, source_target_pairs={{0,4},{4,8},{8,12},{12,16},{16,20},{20,24},{24,28},{28,0},{1,5},{5... | collective-permute-start | bytes 393224 | tf_op jit(solution)/shard_map/ppermute | solution.py:18
  4.8 3.1 %collective-permute-start.1 = (f32[4,16,4,128]{3,2,1,0:T(4,128)S(1)}, f32[4,16,4,128]{3,2,1,0:T(4,128)S(1)}, u32[]{:S(2)}, u32[]{:S(2)}) collective-permute-start(f32[4,16,4,128]{3,2,1,0:T(4,128)S(1)} %get-tuple-element.18), channel_id=1, source_target_pairs={{4,0},{8,4},{12,8},{16,12},{20,16},{24,20},{28,24},{0,28},{5,1},{9... | collective-permute-start | bytes 393224 | tf_op jit(solution)/shard_map/ppermute | solution.py:20
  10.1 3.2 %all-to-all-start = ((s32[4,2,1]{1,2,0:T(1,128)}), s32[4,2,1]{1,2,0:T(1,128)S(1)}, u32[]{:S(2)}, u32[]{:S(2)}) async-start(s32[4,2,1]{1,2,0:T(1,128)} %bitcast.10), calls=%async_computation | async-start | bytes 4096 | tf_op jit(solution)/shard_map/all_to_all | solution.py:93
  15.1 1.2 scatter_custom_fusion.1
  17.0 3.2 %all-to-all-start.1 = ((f32[4,2,128]{2,1,0:T(2,128)}), f32[4,2,128]{2,1,0:T(2,128)S(1)}, u32[]{:S(2)}, u32[]{:S(2)}) async-start(f32[4,2,128]{2,1,0:T(2,128)} %bitcast.18), calls=%async_computation.1 | async-start | bytes 8192 | tf_op jit(solution)/shard_map/all_to_all | solution.py:104
  20.4 3.6 %all-to-all-done.1 = f32[4,2,128]{2,1,0:T(2,128)S(1)} async-done(((f32[4,2,128]{2,1,0:T(2,128)}), f32[4,2,128]{2,1,0:T(2,128)S(1)}, u32[]{:S(2)}, u32[]{:S(2)}) %all-to-all-start.1) | async-done | bytes 4128 | tf_op jit(solution)/shard_map/all_to_all | solution.py:104
  24.8 4.7 %collective-permute-start.5 = (f32[16,4,128]{2,1,0:T(4,128)S(1)}, f32[16,4,128]{2,1,0:T(4,128)}, u32[]{:S(2)}, u32[]{:S(2)}) collective-permute-start(f32[16,4,128]{2,1,0:T(4,128)S(1)} %get-tuple-element.44), channel_id=1, source_target_pairs={{4,0},{8,4},{12,8},{16,12},{20,16},{24,20},{28,24},{0,28},{5,1},{9... | collective-permute-start | bytes 98312 | tf_op jit(solution)/shard_map/ppermute | solution.py:20
  29.5 2.0 collective-permute-done.4
  31.5 0.8 pad_maximum_fusion.2
  32.3 0.8 fusion.137
  33.1 1.7 collective-permute-start.7
  36.3 1.8 collective-permute-start.3
  38.0 2.5 collective-permute-done.6
  40.5 1.3 maximum_multiply_fusion
  41.9 1.3 collective-permute-done.2
  43.7 1.4 copy.27
  45.0 1.0 pad_maximum_fusion
  46.7 0.9 fusion.81
  47.6 1.0 fusion.76
  48.6 1.0 fusion.71
  50.2 4.8 %collective-permute-start.9 = (f32[16,4,128]{2,1,0:T(4,128)S(1)}, f32[16,4,128]{2,1,0:T(4,128)S(1)}, u32[]{:S(2)}, u32[]{:S(2)}) collective-permute-start(f32[16,4,128]{2,1,0:T(4,128)S(1)} %get-tuple-element.42), channel_id=1, source_target_pairs={{4,0},{8,4},{12,8},{16,12},{20,16},{24,20},{28,24},{0,28},{5,1},{9... | collective-permute-start | bytes 98312 | tf_op jit(solution)/shard_map/ppermute | solution.py:20
  54.9 1.8 collective-permute-done.8
  57.0 1.7 collective-permute-start.11
  58.7 5.1 %collective-permute-done.10 = f32[16,24,4]{2,1,0:T(8,128)S(1)} collective-permute-done((f32[16,24,4]{2,1,0:T(8,128)S(1)}, f32[16,24,4]{2,1,0:T(8,128)S(1)}, u32[]{:S(2)}, u32[]{:S(2)}) %collective-permute-start.10) | collective-permute-done | bytes 6176 | tf_op jit(solution)/shard_map/ppermute | solution.py:18
  64.2 1.0 fusion.66
  65.2 1.0 fusion.61
  66.3 1.0 fusion.56
  67.7 1.1 gather_fusion
  68.9 3.2 %all-to-all-start.2 = ((f32[4,2,128]{2,1,0:T(2,128)}), f32[4,2,128]{2,1,0:T(2,128)S(1)}, u32[]{:S(2)}, u32[]{:S(2)}) async-start(f32[4,2,128]{2,1,0:T(2,128)} %bitcast.22), calls=%async_computation.2 | async-start | bytes 8192 | tf_op jit(solution)/shard_map/all_to_all | solution.py:141
  72.1 3.7 %all-to-all-done.2 = f32[4,2,128]{2,1,0:T(2,128)S(1)} async-done(((f32[4,2,128]{2,1,0:T(2,128)}), f32[4,2,128]{2,1,0:T(2,128)S(1)}, u32[]{:S(2)}, u32[]{:S(2)}) %all-to-all-start.2) | async-done | bytes 4128 | tf_op jit(solution)/shard_map/all_to_all | solution.py:141
  76.4 0.9 fusion.6
  78.6 6.1 %all_to_all.69 = f32[4,2,128]{2,1,0:T(2,128)S(1)} all-to-all(f32[4,2,128]{2,1,0:T(2,128)S(1)} %bitcast.119), channel_id=1, replica_groups=mesh['lat'=8,'lon'=4] {'lon'}, dimensions={0} | all-to-all | bytes 8192 | tf_op jit(solution)/shard_map/all_to_all | solution.py:104
  85.5 4.8 %collective-permute-start.13 = (f32[16,4,128]{2,1,0:T(4,128)S(1)}, f32[16,4,128]{2,1,0:T(4,128)S(1)}, u32[]{:S(2)}, u32[]{:S(2)}) collective-permute-start(f32[16,4,128]{2,1,0:T(4,128)S(1)} %get-tuple-element.40), channel_id=1, source_target_pairs={{4,0},{8,4},{12,8},{16,12},{20,16},{24,20},{28,24},{0,28},{5,1},{9... | collective-permute-start | bytes 98312 | tf_op jit(solution)/shard_map/ppermute | solution.py:20
  90.3 1.8 collective-permute-done.12
  92.3 1.7 collective-permute-start.15
  94.1 5.1 %collective-permute-done.14 = f32[16,24,4]{2,1,0:T(8,128)S(1)} collective-permute-done((f32[16,24,4]{2,1,0:T(8,128)S(1)}, f32[16,24,4]{2,1,0:T(8,128)S(1)}, u32[]{:S(2)}, u32[]{:S(2)}) %collective-permute-start.14) | collective-permute-done | bytes 6176 | tf_op jit(solution)/shard_map/ppermute | solution.py:18
  99.5 0.9 fusion.51
  100.4 1.0 fusion.46
  101.4 1.0 fusion.41
  102.5 1.0 multiply_reduce_fusion.2
  103.5 39.0 %all-reduce = (f32[]{:T(128)}, f32[]{:T(128)}) all-reduce(f32[]{:T(128)} %get-tuple-element.5, f32[]{:T(128)} %get-tuple-element.4), channel_id=1, replica_groups=mesh['lat'=8,'lon'=4] {'lat','lon'}, use_global_device_ids=true, to_apply=%region_6.7 | all-reduce | flops 2 | bytes 16 | tf_op jit(solution)/shard_map/psum | solution.py:116
  144.5 42.3 %psum.30 = f32[]{:T(128)} all-reduce(f32[]{:T(128)} %multiply_reduce_fusion.1), channel_id=1, replica_groups=mesh['lat'=8,'lon'=4] {'lat','lon'}, use_global_device_ids=true, to_apply=%region_12.13 | all-reduce | flops 1 | bytes 8 | tf_op jit(solution)/shard_map/psum | solution.py:116
  188.2 2.3 collective-permute-start.16
  190.5 2.4 collective-permute-start.17
  192.9 1.9 collective-permute-done.16
  195.0 1.7 collective-permute-start.19
  196.8 3.3 %collective-permute-done.18 = f32[16,24,4]{2,1,0:T(8,128)S(1)} collective-permute-done((f32[16,24,4]{2,1,0:T(8,128)S(1)}, f32[16,24,4]{2,1,0:T(8,128)S(1)}, u32[]{:S(2)}, u32[]{:S(2)}) %collective-permute-start.18) | collective-permute-done | bytes 6176 | tf_op jit(solution)/shard_map/ppermute | solution.py:18
  200.1 1.8 collective-permute-done.19
  202.2 1.0 fusion.36
  203.3 1.0 fusion.31
  204.3 1.0 fusion.26
  206.3 7.5 %all_to_all.70 = f32[4,2,128]{2,1,0:T(2,128)S(1)} all-to-all(f32[4,2,128]{2,1,0:T(2,128)S(1)} %bitcast.117), channel_id=1, replica_groups=mesh['lat'=8,'lon'=4] {'lon'}, dimensions={0} | all-to-all | bytes 8192 | tf_op jit(solution)/shard_map/all_to_all | solution.py:141
  214.4 0.9 fusion.2
  216.5 6.1 %all_to_all.71 = f32[4,2,128]{2,1,0:T(2,128)S(1)} all-to-all(f32[4,2,128]{2,1,0:T(2,128)S(1)} %bitcast.118), channel_id=1, replica_groups=mesh['lat'=8,'lon'=4] {'lon'}, dimensions={0} | all-to-all | bytes 8192 | tf_op jit(solution)/shard_map/all_to_all | solution.py:104
  223.4 4.8 %collective-permute-start.21 = (f32[16,4,128]{2,1,0:T(4,128)S(1)}, f32[16,4,128]{2,1,0:T(4,128)S(1)}, u32[]{:S(2)}, u32[]{:S(2)}) collective-permute-start(f32[16,4,128]{2,1,0:T(4,128)S(1)} %get-tuple-element.36), channel_id=1, source_target_pairs={{4,0},{8,4},{12,8},{16,12},{20,16},{24,20},{28,24},{0,28},{5,1},{9... | collective-permute-start | bytes 98312 | tf_op jit(solution)/shard_map/ppermute | solution.py:20
  228.2 1.8 collective-permute-done.20
  230.2 1.7 collective-permute-start.23
  232.0 5.1 %collective-permute-done.22 = f32[16,24,4]{2,1,0:T(8,128)S(1)} collective-permute-done((f32[16,24,4]{2,1,0:T(8,128)S(1)}, f32[16,24,4]{2,1,0:T(8,128)S(1)}, u32[]{:S(2)}, u32[]{:S(2)}) %collective-permute-start.22) | collective-permute-done | bytes 6176 | tf_op jit(solution)/shard_map/ppermute | solution.py:18
  237.4 0.9 fusion.21
  238.3 1.0 fusion.16
  239.3 1.0 fusion.11
  240.3 1.0 multiply_reduce_fusion
  241.3 38.9 %psum.31 = f32[]{:T(128)} all-reduce(f32[]{:T(128)} %get-tuple-element.8), channel_id=1, replica_groups=mesh['lat'=8,'lon'=4] {'lat','lon'}, use_global_device_ids=true, to_apply=%region_16.17 | all-reduce | flops 1 | bytes 8 | tf_op jit(solution)/shard_map/psum | solution.py:158
  (111 shorter events, 17.7 us)
Async XLA Ops:
  0.6 13.9 %copy-start = (f32[1,8,128,128]{3,2,1,0:T(8,128)S(1)}, f32[1,8,128,128]{3,2,1,0:T(8,128)}, u32[]{:S(2)}) copy-start(f32[1,8,128,128]{3,2,1,0:T(8,128)} %param.8) | copy-start | bytes 1572868
  0.6 7.3 %copy-start.9 = (s32[1,8,1]{1,2,0:T(1,128)S(1)}, s32[1,8,1]{1,2,0:T(1,128)}, u32[]{:S(2)}) copy-start(s32[1,8,1]{1,2,0:T(1,128)} %param.11) | copy-start | bytes 100
  0.7 8.2 %copy-start.12 = (s32[1,8]{1,0:T(1,128)S(1)}, s32[1,8]{1,0:T(1,128)}, u32[]{:S(2)}) copy-start(s32[1,8]{1,0:T(1,128)} %param.12) | copy-start | bytes 100
  0.7 13.8 %copy-start.6 = (f32[1,8,128]{2,1,0:T(8,128)S(1)}, f32[1,8,128]{2,1,0:T(8,128)}, u32[]{:S(2)}) copy-start(f32[1,8,128]{2,1,0:T(8,128)} %param.10) | copy-start | bytes 12292
  0.7 13.8 %copy-start.1 = (f32[1,8,128]{2,1,0:T(8,128)S(1)}, f32[1,8,128]{2,1,0:T(8,128)}, u32[]{:S(2)}) copy-start(f32[1,8,128]{2,1,0:T(8,128)} %param.9) | copy-start | bytes 12292
  1.8 33.0 %collective-permute-start = (f32[4,16,4,128]{3,2,1,0:T(4,128)S(1)}, f32[4,16,4,128]{3,2,1,0:T(4,128)S(1)}, u32[]{:S(2)}, u32[]{:S(2)}) collective-permute-start(f32[4,16,4,128]{3,2,1,0:T(4,128)S(1)} %get-tuple-element.17), channel_id=1, source_target_pairs={{0,4},{4,8},{8,12},{12,16},{16,20},{20,24},{24,28},{28,0},{1,5},{5... | collective-permute-start | bytes 393224 | tf_op jit(solution)/shard_map/ppermute | solution.py:18
  4.8 30.0 %collective-permute-start.1 = (f32[4,16,4,128]{3,2,1,0:T(4,128)S(1)}, f32[4,16,4,128]{3,2,1,0:T(4,128)S(1)}, u32[]{:S(2)}, u32[]{:S(2)}) collective-permute-start(f32[4,16,4,128]{3,2,1,0:T(4,128)S(1)} %get-tuple-element.18), channel_id=1, source_target_pairs={{4,0},{8,4},{12,8},{16,12},{20,16},{24,20},{28,24},{0,28},{5,1},{9... | collective-permute-start | bytes 393224 | tf_op jit(solution)/shard_map/ppermute | solution.py:20
  8.2 15.9 %copy-start.10 = (s32[8]{0:T(128)}, s32[8]{0:T(128)S(1)}, u32[]{:S(2)}) copy-start(s32[8]{0:T(128)S(1)} %fusion.127) | copy-start | bytes 100
  10.1 6.9 %all-to-all-start = ((s32[4,2,1]{1,2,0:T(1,128)}), s32[4,2,1]{1,2,0:T(1,128)S(1)}, u32[]{:S(2)}, u32[]{:S(2)}) async-start(s32[4,2,1]{1,2,0:T(1,128)} %bitcast.10), calls=%async_computation | async-start | bytes 4096 | tf_op jit(solution)/shard_map/all_to_all | solution.py:93
  14.4 2.6 copy-start.4
  17.0 7.0 %all-to-all-start.1 = ((f32[4,2,128]{2,1,0:T(2,128)}), f32[4,2,128]{2,1,0:T(2,128)S(1)}, u32[]{:S(2)}, u32[]{:S(2)}) async-start(f32[4,2,128]{2,1,0:T(2,128)} %bitcast.18), calls=%async_computation.1 | async-start | bytes 8192 | tf_op jit(solution)/shard_map/all_to_all | solution.py:104
  20.4 4.3 %copy-start.7 = (s32[8]{0:T(128)}, s32[8]{0:T(128)S(1)}, u32[]{:S(2)}) copy-start(s32[8]{0:T(128)S(1)} %reshape.175) | copy-start | bytes 100
  24.7 6.8 %collective-permute-start.4 = (f32[16,4,128]{2,1,0:T(4,128)S(1)}, f32[16,4,128]{2,1,0:T(4,128)}, u32[]{:S(2)}, u32[]{:S(2)}) collective-permute-start(f32[16,4,128]{2,1,0:T(4,128)S(1)} %get-tuple-element.43), channel_id=1, source_target_pairs={{0,4},{4,8},{8,12},{12,16},{16,20},{20,24},{24,28},{28,0},{1,5},{5... | collective-permute-start | bytes 98312 | tf_op jit(solution)/shard_map/ppermute | solution.py:18
  24.8 6.7 %collective-permute-start.5 = (f32[16,4,128]{2,1,0:T(4,128)S(1)}, f32[16,4,128]{2,1,0:T(4,128)}, u32[]{:S(2)}, u32[]{:S(2)}) collective-permute-start(f32[16,4,128]{2,1,0:T(4,128)S(1)} %get-tuple-element.44), channel_id=1, source_target_pairs={{4,0},{8,4},{12,8},{16,12},{20,16},{24,20},{28,24},{0,28},{5,1},{9... | collective-permute-start | bytes 98312 | tf_op jit(solution)/shard_map/ppermute | solution.py:20
  33.1 7.4 %collective-permute-start.6 = (f32[16,24,4]{2,1,0:T(8,128)}, f32[16,24,4]{2,1,0:T(8,128)}, u32[]{:S(2)}, u32[]{:S(2)}) collective-permute-start(f32[16,24,4]{2,1,0:T(8,128)} %get-tuple-element.31), channel_id=1, source_target_pairs={{0,1},{1,2},{2,3},{3,0},{4,5},{5,6},{6,7},{7,4},{8,9},{9,10},{10,1... | collective-permute-start | bytes 18440 | tf_op jit(solution)/shard_map/ppermute | solution.py:18
  33.1 7.4 %collective-permute-start.7 = (f32[16,24,4]{2,1,0:T(8,128)S(1)}, f32[16,24,4]{2,1,0:T(8,128)}, u32[]{:S(2)}, u32[]{:S(2)}) collective-permute-start(f32[16,24,4]{2,1,0:T(8,128)S(1)} %get-tuple-element.32), channel_id=1, source_target_pairs={{1,0},{2,1},{3,2},{0,3},{5,4},{6,5},{7,6},{4,7},{9,8},{10,9},{11,1... | collective-permute-start | bytes 18440 | tf_op jit(solution)/shard_map/ppermute | solution.py:20
  35.7 7.5 %collective-permute-start.2 = (f32[4,16,24,4]{2,1,3,0:T(8,128)S(1)}, f32[4,16,24,4]{2,1,3,0:T(8,128)S(1)}, u32[]{:S(2)}, u32[]{:S(2)}) collective-permute-start(f32[4,16,24,4]{2,1,3,0:T(8,128)S(1)} %copy.24), channel_id=1, source_target_pairs={{0,1},{1,2},{2,3},{3,0},{4,5},{5,6},{6,7},{7,4},{8,9},{9,10},{10,1... | collective-permute-start | bytes 73736 | tf_op jit(solution)/shard_map/ppermute | solution.py:18
  36.3 7.4 %collective-permute-start.3 = (f32[4,16,24,4]{2,1,3,0:T(8,128)S(1)}, f32[4,16,24,4]{2,1,3,0:T(8,128)}, u32[]{:S(2)}, u32[]{:S(2)}) collective-permute-start(f32[4,16,24,4]{2,1,3,0:T(8,128)S(1)} %copy.25), channel_id=1, source_target_pairs={{1,0},{2,1},{3,2},{0,3},{5,4},{6,5},{7,6},{4,7},{9,8},{10,9},{11,1... | collective-permute-start | bytes 73736 | tf_op jit(solution)/shard_map/ppermute | solution.py:20
  46.1 0.6 copy-start.3
  46.7 0.9 copy-start.2
  49.6 9.1 %copy-start.8 = (s32[8]{0:T(128)S(1)}, s32[8]{0:T(128)}, u32[]{:S(2)}) copy-start(s32[8]{0:T(128)} %copy-done.7) | copy-start | bytes 100
  50.1 6.7 %collective-permute-start.8 = (f32[16,4,128]{2,1,0:T(4,128)S(1)}, f32[16,4,128]{2,1,0:T(4,128)S(1)}, u32[]{:S(2)}, u32[]{:S(2)}) collective-permute-start(f32[16,4,128]{2,1,0:T(4,128)S(1)} %get-tuple-element.41), channel_id=1, source_target_pairs={{0,4},{4,8},{8,12},{12,16},{16,20},{20,24},{24,28},{28,0},{1,5},{5... | collective-permute-start | bytes 98312 | tf_op jit(solution)/shard_map/ppermute | solution.py:18
  50.2 6.6 %collective-permute-start.9 = (f32[16,4,128]{2,1,0:T(4,128)S(1)}, f32[16,4,128]{2,1,0:T(4,128)S(1)}, u32[]{:S(2)}, u32[]{:S(2)}) collective-permute-start(f32[16,4,128]{2,1,0:T(4,128)S(1)} %get-tuple-element.42), channel_id=1, source_target_pairs={{4,0},{8,4},{12,8},{16,12},{20,16},{24,20},{28,24},{0,28},{5,1},{9... | collective-permute-start | bytes 98312 | tf_op jit(solution)/shard_map/ppermute | solution.py:20
  56.9 7.0 %collective-permute-start.10 = (f32[16,24,4]{2,1,0:T(8,128)S(1)}, f32[16,24,4]{2,1,0:T(8,128)S(1)}, u32[]{:S(2)}, u32[]{:S(2)}) collective-permute-start(f32[16,24,4]{2,1,0:T(8,128)S(1)} %get-tuple-element.29), channel_id=1, source_target_pairs={{0,1},{1,2},{2,3},{3,0},{4,5},{5,6},{6,7},{7,4},{8,9},{9,10},{10,1... | collective-permute-start | bytes 18440 | tf_op jit(solution)/shard_map/ppermute | solution.py:18
  57.0 6.9 %collective-permute-start.11 = (f32[16,24,4]{2,1,0:T(8,128)S(1)}, f32[16,24,4]{2,1,0:T(8,128)S(1)}, u32[]{:S(2)}, u32[]{:S(2)}) collective-permute-start(f32[16,24,4]{2,1,0:T(8,128)S(1)} %get-tuple-element.30), channel_id=1, source_target_pairs={{1,0},{2,1},{3,2},{0,3},{5,4},{6,5},{7,6},{4,7},{9,8},{10,9},{11,1... | collective-permute-start | bytes 18440 | tf_op jit(solution)/shard_map/ppermute | solution.py:20
  66.3 5.9 %copy-start.11 = (s32[8]{0:T(128)S(1)}, s32[8]{0:T(128)}, u32[]{:S(2)}) copy-start(s32[8]{0:T(128)} %copy-done.10) | copy-start | bytes 100
  67.3 10.1 %copy-start.5 = (pred[8]{0:T(512)(128)(4,1)S(1)}, pred[8]{0:T(512)(128)(4,1)}, u32[]{:S(2)}) copy-start(pred[8]{0:T(512)(128)(4,1)} %copy-done.4) | copy-start | bytes 28
  68.9 7.0 %all-to-all-start.2 = ((f32[4,2,128]{2,1,0:T(2,128)}), f32[4,2,128]{2,1,0:T(2,128)S(1)}, u32[]{:S(2)}, u32[]{:S(2)}) async-start(f32[4,2,128]{2,1,0:T(2,128)} %bitcast.22), calls=%async_computation.2 | async-start | bytes 8192 | tf_op jit(solution)/shard_map/all_to_all | solution.py:141
  85.4 6.7 %collective-permute-start.12 = (f32[16,4,128]{2,1,0:T(4,128)S(1)}, f32[16,4,128]{2,1,0:T(4,128)S(1)}, u32[]{:S(2)}, u32[]{:S(2)}) collective-permute-start(f32[16,4,128]{2,1,0:T(4,128)S(1)} %get-tuple-element.39), channel_id=1, source_target_pairs={{0,4},{4,8},{8,12},{12,16},{16,20},{20,24},{24,28},{28,0},{1,5},{5... | collective-permute-start | bytes 98312 | tf_op jit(solution)/shard_map/ppermute | solution.py:18
  85.5 6.7 %collective-permute-start.13 = (f32[16,4,128]{2,1,0:T(4,128)S(1)}, f32[16,4,128]{2,1,0:T(4,128)S(1)}, u32[]{:S(2)}, u32[]{:S(2)}) collective-permute-start(f32[16,4,128]{2,1,0:T(4,128)S(1)} %get-tuple-element.40), channel_id=1, source_target_pairs={{4,0},{8,4},{12,8},{16,12},{20,16},{24,20},{28,24},{0,28},{5,1},{9... | collective-permute-start | bytes 98312 | tf_op jit(solution)/shard_map/ppermute | solution.py:20
  92.3 6.9 %collective-permute-start.14 = (f32[16,24,4]{2,1,0:T(8,128)S(1)}, f32[16,24,4]{2,1,0:T(8,128)S(1)}, u32[]{:S(2)}, u32[]{:S(2)}) collective-permute-start(f32[16,24,4]{2,1,0:T(8,128)S(1)} %get-tuple-element.27), channel_id=1, source_target_pairs={{0,1},{1,2},{2,3},{3,0},{4,5},{5,6},{6,7},{7,4},{8,9},{9,10},{10,1... | collective-permute-start | bytes 18440 | tf_op jit(solution)/shard_map/ppermute | solution.py:18
  92.3 6.9 %collective-permute-start.15 = (f32[16,24,4]{2,1,0:T(8,128)S(1)}, f32[16,24,4]{2,1,0:T(8,128)S(1)}, u32[]{:S(2)}, u32[]{:S(2)}) collective-permute-start(f32[16,24,4]{2,1,0:T(8,128)S(1)} %get-tuple-element.28), channel_id=1, source_target_pairs={{1,0},{2,1},{3,2},{0,3},{5,4},{6,5},{7,6},{4,7},{9,8},{10,9},{11,1... | collective-permute-start | bytes 18440 | tf_op jit(solution)/shard_map/ppermute | solution.py:20
  188.2 6.7 %collective-permute-start.16 = (f32[16,4,128]{2,1,0:T(4,128)S(1)}, f32[16,4,128]{2,1,0:T(4,128)S(1)}, u32[]{:S(2)}, u32[]{:S(2)}) collective-permute-start(f32[16,4,128]{2,1,0:T(4,128)S(1)} %get-tuple-element.37), channel_id=1, source_target_pairs={{0,4},{4,8},{8,12},{12,16},{16,20},{20,24},{24,28},{28,0},{1,5},{5... | collective-permute-start | bytes 98312 | tf_op jit(solution)/shard_map/ppermute | solution.py:18
  190.5 4.3 %collective-permute-start.17 = (f32[16,4,128]{2,1,0:T(4,128)S(1)}, f32[16,4,128]{2,1,0:T(4,128)S(1)}, u32[]{:S(2)}, u32[]{:S(2)}) collective-permute-start(f32[16,4,128]{2,1,0:T(4,128)S(1)} %get-tuple-element.38), channel_id=1, source_target_pairs={{4,0},{8,4},{12,8},{16,12},{20,16},{24,20},{28,24},{0,28},{5,1},{9... | collective-permute-start | bytes 98312 | tf_op jit(solution)/shard_map/ppermute | solution.py:20
  195.0 5.1 %collective-permute-start.18 = (f32[16,24,4]{2,1,0:T(8,128)S(1)}, f32[16,24,4]{2,1,0:T(8,128)S(1)}, u32[]{:S(2)}, u32[]{:S(2)}) collective-permute-start(f32[16,24,4]{2,1,0:T(8,128)S(1)} %get-tuple-element.25), channel_id=1, source_target_pairs={{0,1},{1,2},{2,3},{3,0},{4,5},{5,6},{6,7},{7,4},{8,9},{9,10},{10,1... | collective-permute-start | bytes 18440 | tf_op jit(solution)/shard_map/ppermute | solution.py:18
  195.0 6.9 %collective-permute-start.19 = (f32[16,24,4]{2,1,0:T(8,128)S(1)}, f32[16,24,4]{2,1,0:T(8,128)S(1)}, u32[]{:S(2)}, u32[]{:S(2)}) collective-permute-start(f32[16,24,4]{2,1,0:T(8,128)S(1)} %get-tuple-element.26), channel_id=1, source_target_pairs={{1,0},{2,1},{3,2},{0,3},{5,4},{6,5},{7,6},{4,7},{9,8},{10,9},{11,1... | collective-permute-start | bytes 18440 | tf_op jit(solution)/shard_map/ppermute | solution.py:20
  223.3 6.7 %collective-permute-start.20 = (f32[16,4,128]{2,1,0:T(4,128)S(1)}, f32[16,4,128]{2,1,0:T(4,128)S(1)}, u32[]{:S(2)}, u32[]{:S(2)}) collective-permute-start(f32[16,4,128]{2,1,0:T(4,128)S(1)} %get-tuple-element.35), channel_id=1, source_target_pairs={{0,4},{4,8},{8,12},{12,16},{16,20},{20,24},{24,28},{28,0},{1,5},{5... | collective-permute-start | bytes 98312 | tf_op jit(solution)/shard_map/ppermute | solution.py:18
  223.4 6.6 %collective-permute-start.21 = (f32[16,4,128]{2,1,0:T(4,128)S(1)}, f32[16,4,128]{2,1,0:T(4,128)S(1)}, u32[]{:S(2)}, u32[]{:S(2)}) collective-permute-start(f32[16,4,128]{2,1,0:T(4,128)S(1)} %get-tuple-element.36), channel_id=1, source_target_pairs={{4,0},{8,4},{12,8},{16,12},{20,16},{24,20},{28,24},{0,28},{5,1},{9... | collective-permute-start | bytes 98312 | tf_op jit(solution)/shard_map/ppermute | solution.py:20
  230.2 6.9 %collective-permute-start.22 = (f32[16,24,4]{2,1,0:T(8,128)S(1)}, f32[16,24,4]{2,1,0:T(8,128)S(1)}, u32[]{:S(2)}, u32[]{:S(2)}) collective-permute-start(f32[16,24,4]{2,1,0:T(8,128)S(1)} %get-tuple-element.23), channel_id=1, source_target_pairs={{0,1},{1,2},{2,3},{3,0},{4,5},{5,6},{6,7},{7,4},{8,9},{9,10},{10,1... | collective-permute-start | bytes 18440 | tf_op jit(solution)/shard_map/ppermute | solution.py:18
  230.2 6.9 %collective-permute-start.23 = (f32[16,24,4]{2,1,0:T(8,128)S(1)}, f32[16,24,4]{2,1,0:T(8,128)S(1)}, u32[]{:S(2)}, u32[]{:S(2)}) collective-permute-start(f32[16,24,4]{2,1,0:T(8,128)S(1)} %get-tuple-element.24), channel_id=1, source_target_pairs={{1,0},{2,1},{3,2},{0,3},{5,4},{6,5},{7,6},{4,7},{9,8},{10,9},{11,1... | collective-permute-start | bytes 18440 | tf_op jit(solution)/shard_map/ppermute | solution.py:20
where the time goes:
time: 284 us; the launch traced here: 282 us
  blocking collectives  140 us (49%)
  starting transfers between devices  50.7 us (18%)
  waiting for transfers between devices  41.9 us (15%)
  other arithmetic  28.9 us (10%)
  local copies, waits for them, and re-layouts  11.5 us (4%)
  between operations  5.88 us (2%)
  matrix products  3.45 us (1%)
    psum x2, blocking collectives, squares(): return lax.psum(jnp.sum(vector * vector), ('lat', 'lon'))  81.3 us
    psum x1, blocking collectives, shards(): lax.psum(jnp.sum(direction * image_vec), ('lat', 'lon'))  38.9 us
    ppermute x12, starting transfers between devices, padded_2(): lax.ppermute(head, axis, [((i + 1) % count, i) for i in range(count)])  35.1 us
    ppermute x12, waiting for transfers between devices, padded_2(): lax.ppermute(tail, axis, [(i, (i + 1) % count) for i in range(count)])  31.9 us
    all_to_all x2, blocking collectives, to_owner(): lax.all_to_all(outgoing, 'lon', split_axis=0, concat_axis=0, tiled=True)  12.3 us
    mul x10, other arithmetic, model_adjoint(): padded = fresh_field * edge_mask(margin)  9.2 us
    all_to_all x1, blocking collectives, shards(): lax.all_to_all(state_rows[asked_rows], 'lon', split_axis=0, concat_axis=0...  7.5 us
    mul x8, other arithmetic, shards(): model_padded = model_fresh_field * edge_mask(model_margin)  7.01 us
  transfers between devices with their start and end apart: 27, of which 15 were waited for; matrix products, arithmetic and copies ran while one was open for 3% of the time, Pallas kernels for 0%

commit v1 on v0

v1 whole, which is shorter than its diff:
```python
import functools

import jax
import jax.numpy as jnp
from jax import lax
from jax.experimental import pallas as pl
from jax.experimental.pallas import tpu as pltpu
from jax.sharding import PartitionSpec as P

STEPS = 4
HALO = 2 * STEPS
MESH = pl.DeviceIdType.MESH
F32 = jnp.float32
BF16 = jnp.bfloat16


def split3(x):
    hi = x.astype(BF16)
    rest = x - hi.astype(F32)
    mid = rest.astype(BF16)
    low = (rest - mid.astype(F32)).astype(BF16)
    return hi, mid, low


def dot3(onehot, x):
    total = None
    for part in split3(x):
        term = jnp.dot(onehot, part, preferred_element_type=F32)
        total = term if total is None else total + term
    return total


def kernel(
    n_lat, n_lon,
    courant, obs, weight, innov, owner, row, count,
    inc_out, res_out,
    rate_in, rates, obs_v, terms, codes, code_out, spread_mat, gather_mat,
    field, moved, parts_t, parts_o, fetch_out, fetch_in, red_lon, red_lat,
    obs_sem, own_sem, wide_send, wide_recv, fetch_send, fetch_recv, part_send, part_recv,
    lon_send, lon_recv, lat_send, lat_recv,
):
    li = lax.axis_index("lat")
    lo = lax.axis_index("lon")
    levels, clat, clon = inc_out.shape
    cap = obs_v.shape[0]
    share = levels // n_lon
    ext = clat + 2 * HALO
    tile_rows = n_lon * ext
    n_src = 3 * n_lon

    obs_copy = pltpu.make_async_copy(obs.at[0], obs_v, obs_sem)
    obs_copy.start()

    def exists(d):
        return (li + d >= 0) & (li + d < n_lat)

    def guarded(d, run):
        if d == 0:
            run()
        else:
            pl.when(exists(d))(run)

    pairs = [(d, j) for d in (-1, 1, 0) for j in range(n_lon) if (d, j) != (0, 0)]

    def lon_at(j):
        return lax.rem(lo + j + n_lon, n_lon)

    barrier = pltpu.get_barrier_semaphore()

    def greet(lat, lon):
        pl.semaphore_signal(barrier, inc=1, device_id={"lat": lat, "lon": lon}, device_id_type=MESH)

    for d in (-1, 1):
        def hello(d=d):
            for j in range(1, n_lon):
                greet(li + d, lon_at(j))
        guarded(d, hello)
    for j in range(1, n_lon):
        greet(li, lon_at(j))

    @pl.loop(1, n_lat)
    def _(j):
        greet(lax.rem(li + j, n_lat), lo)

    sub = lax.broadcasted_iota(jnp.int32, (cap, clon), 0)
    live = count[0, 0]
    scal = []
    for b in range(cap):
        r = row[0, b]
        lev = lax.div(r, jnp.int32(clat))
        scal.append((r - lev * clat, (lev * n_lon + owner[0, b, 0]) * ext))
    for d in (-1, 0, 1):
        tile = jnp.full((cap, clon), -1, jnp.int32)
        for b in range(cap):
            lat_local = scal[b][0] + (HALO - clat * d)
            ok = (lat_local >= 0) & (lat_local < ext) & (b < live)
            tile = jnp.where(sub == b, jnp.where(ok, scal[b][1] + lat_local, -1), tile)
        code_out[d + 1] = tile.astype(F32)

    sides = (li > 0).astype(jnp.int32) + (li < n_lat - 1).astype(jnp.int32)
    pl.semaphore_wait(barrier, (n_lon - 1) + (n_lat - 1) + sides * (n_lon - 1))

    def wide(kind, d, j, src, dst):
        return pltpu.make_async_remote_copy(
            src_ref=src, dst_ref=dst,
            send_sem=wide_send.at[kind, d + 1, j], recv_sem=wide_recv.at[kind, d + 1, j],
            device_id={"lat": li + d, "lon": lon_at(j)}, device_id_type=MESH,
        )

    def send_slot(d):
        return (1 - d) * n_lon + lo

    def recv_slot(d, j):
        return (1 - d) * n_lon + lon_at(-j)

    def code_copy(d, j, slot):
        return wide(0, d, j, code_out.at[d + 1], codes.at[slot])

    def rate_copy(d, j, peer, tile):
        levs = pl.ds(peer * share, share)
        if d == 0:
            src, dst = pl.ds(0, clat), pl.ds(HALO, clat)
        elif d == 1:
            src, dst = pl.ds(clat - HALO, HALO), pl.ds(0, HALO)
        else:
            src, dst = pl.ds(0, HALO), pl.ds(HALO + clat, HALO)
        return wide(1, d, j, courant.at[:, levs, src, :], rate_in.at[:, :, tile, dst, :])

    def term_copy(rnd, d, j, slot):
        return wide(2 + rnd, d, j, terms.at[rnd, n_lon + lo], terms.at[rnd, slot])

    def start_wide(make):
        for d in (-1, 1, 0):
            def run(d=d):
                for j in range(n_lon):
                    if (d, j) != (0, 0):
                        make(d, j, True).start()
            guarded(d, run)

    def recv_wide(make):
        for d in (-1, 1, 0):
            def run(d=d):
                for j in range(n_lon):
                    if (d, j) != (0, 0):
                        make(d, j, False).wait_recv()
            guarded(-d, run)

    def done_wide(make):
        for d in (-1, 1, 0):
            def run(d=d):
                for j in range(n_lon):
                    if (d, j) != (0, 0):
                        make(d, j, True).wait_send()
            guarded(d, run)

    def code_make(d, j, out):
        return code_copy(d, j, send_slot(d) if out else recv_slot(d, j))

    def rate_make(d, j, out):
        return rate_copy(d, j, lon_at(j), lo if out else lon_at(-j))

    def term_make(rnd):
        return lambda d, j, out: term_copy(rnd, d, j, send_slot(d) if out else recv_slot(d, j))

    own_rate = pltpu.make_async_copy(
        courant.at[:, pl.ds(lo * share, share), :, :],
        rate_in.at[:, :, lo, pl.ds(HALO, clat), :], own_sem)
    start_wide(rate_make)
    start_wide(code_make)
    own_rate.start()
    codes[n_lon + lo] = code_out[1]

    pad = codes.shape[0] - n_src
    none = jnp.full((n_lon, cap, clon), -1.0, F32)
    if pad:
        codes[n_src:] = jnp.full((pad, cap, clon), -1.0, F32)
        for rnd in range(3):
            terms[rnd, n_src:] = jnp.zeros((pad, cap, clon), F32)
    for d in (-1, 1):
        @pl.when(jnp.logical_not(exists(d)))
        def _(d=d):
            first = (d + 1) * n_lon
            codes[first:first + n_lon] = none
            for rnd in range(3):
                terms[rnd, first:first + n_lon] = jnp.zeros((n_lon, cap, clon), F32)
            lat0 = 0 if d == -1 else HALO + clat
            rate_in[:, :, :, lat0:lat0 + HALO, :] = jnp.zeros((2, share, n_lon, HALO, clon), F32)

    live_rows = sub < live
    w_rows = jnp.where(live_rows, weight[0], 0.0)
    wy_rows = w_rows * innov[0]
    stacked = jnp.concatenate([w_rows, wy_rows, jnp.zeros((clon - 2 * cap, clon), F32)], axis=0)
    columns = jnp.transpose(stacked)
    w_col = [columns[:, b:b + 1] for b in range(cap)]

    def spread(rnd, u_cols):
        out = [jnp.sum(obs_v[b] * u_cols[b], axis=0, keepdims=True) for b in range(cap)]
        terms[rnd, n_lon + lo] = jnp.concatenate(out, axis=0)
        start_wide(term_make(rnd))

    obs_copy.wait()
    spread(0, [columns[:, cap + b:cap + b + 1] for b in range(cap)])

    base = (lo * (share * tile_rows)).astype(F32)
    recv_wide(code_make)
    n_blocks = codes.shape[0] * cap
    flat_codes = codes[...].reshape(n_blocks, clon) - base
    code_row = jnp.transpose(flat_codes)[0:1, :]
    for k in range(share):
        place = lax.broadcasted_iota(jnp.int32, (tile_rows, n_blocks), 0).astype(F32) + float(k * tile_rows)
        spread_mat[k * tile_rows:(k + 1) * tile_rows, :] = jnp.where(place == code_row, 1.0, 0.0).astype(BF16)
    centre = flat_codes[n_lon * cap:2 * n_lon * cap, :]
    for c in range(share * tile_rows // clon):
        lane_place = lax.broadcasted_iota(jnp.int32, centre.shape, 1).astype(F32) + float(c * clon)
        gather_mat[:, c * clon:(c + 1) * clon] = jnp.where(lane_place == centre, 1.0, 0.0).astype(BF16)

    recv_wide(rate_make)
    own_rate.wait()
    for k in range(share):
        c0 = rate_in[0, k].reshape(tile_rows, clon)
        c1 = rate_in[1, k].reshape(tile_rows, clon)
        a, b = jnp.maximum(c0, 0.0), jnp.maximum(-c0, 0.0)
        e, f = jnp.maximum(c1, 0.0), jnp.maximum(-c1, 0.0)
        rates[0, k], rates[1, k], rates[2, k], rates[3, k] = a, b, e, f
        rates[4, k] = 1.0 - a - b - e - f

    lane = lax.broadcasted_iota(jnp.int32, (tile_rows, clon), 1)
    lat_ids = lax.broadcasted_iota(jnp.int32, (ext, clon), 0) + (li * clat - HALO)
    inside = jnp.where((lat_ids >= 0) & (lat_ids < n_lat * clat), 1.0, 0.0)
    inside = jnp.concatenate([inside] * n_lon, axis=0)

    def lat_up(x):
        return pltpu.roll(x, tile_rows - 1, 0)

    def lat_down(x):
        return pltpu.roll(x, 1, 0)

    def lon_up(x):
        xs = pltpu.roll(x, clon - 1, 1)
        return jnp.where(lane == clon - 1, jnp.concatenate([xs[ext:], xs[:ext]], axis=0), xs)

    def lon_down(x):
        xs = pltpu.roll(x, 1, 1)
        return jnp.where(lane == 0, jnp.concatenate([xs[-ext:], xs[:-ext]], axis=0), xs)

    def apply_model(rnd, forward):
        flat = dot3(spread_mat[...], terms[rnd].reshape(n_blocks, clon))
        field[...] = flat.reshape(share, tile_rows, clon)

        @pl.loop(0, share)
        def _(k):
            y = field[k]
            for _ in range(STEPS):
                y = (rates[4, k] * y + lat_up(rates[0, k] * y) + lat_down(rates[1, k] * y)
                     + lon_up(rates[2, k] * y) + lon_down(rates[3, k] * y))
            for t in range(n_lon):
                parts_t[rnd, t, k] = y[t * ext + HALO:t * ext + HALO + clat]
            if forward:
                x = y * inside
                for _ in range(STEPS):
                    x = (rates[4, k] * x + rates[0, k] * lat_down(x) + rates[1, k] * lat_up(x)
                         + rates[2, k] * lon_down(x) + rates[3, k] * lon_up(x))
                moved[k] = x

    def part_make(rnd, j, out):
        place = lo if out else lon_at(-j)
        return pltpu.make_async_remote_copy(
            src_ref=parts_t.at[rnd, lon_at(j)],
            dst_ref=parts_o.at[rnd, pl.ds(place * share, share)],
            send_sem=part_send.at[rnd, j], recv_sem=part_recv.at[rnd, j],
            device_id={"lat": li, "lon": lon_at(j)}, device_id_type=MESH)

    def send_parts(rnd):
        for j in range(1, n_lon):
            part_make(rnd, j, True).start()
        parts_o[rnd, pl.ds(lo * share, share)] = parts_t[rnd, lo]

    def fetch_make(rnd, j, out):
        place = lo if out else lon_at(-j)
        return pltpu.make_async_remote_copy(
            src_ref=fetch_out.at[rnd, lon_at(j)], dst_ref=fetch_in.at[rnd, place],
            send_sem=fetch_send.at[rnd, j], recv_sem=fetch_recv.at[rnd, j],
            device_id={"lat": li, "lon": lon_at(j)}, device_id_type=MESH)

    def send_fetch(rnd):
        seen = dot3(gather_mat[...], moved[...].reshape(share * tile_rows, clon))
        fetch_out[rnd] = seen.reshape(n_lon, cap, clon)
        for j in range(1, n_lon):
            fetch_make(rnd, j, True).start()
        fetch_in[rnd, lo] = fetch_out[rnd, lo]

    def observe(rnd):
        for j in range(1, n_lon):
            fetch_make(rnd, j, False).wait_recv()
        seen = jnp.sum(fetch_in[rnd], axis=0)
        return [jnp.sum(obs_v[b] * seen[b:b + 1, :], axis=1, keepdims=True) for b in range(cap)]

    def red_lon_make(rnd, j, out):
        return pltpu.make_async_remote_copy(
            src_ref=red_lon.at[rnd, lo], dst_ref=red_lon.at[rnd, lo if out else lon_at(-j)],
            send_sem=lon_send.at[rnd, j], recv_sem=lon_recv.at[rnd, j],
            device_id={"lat": li, "lon": lon_at(j)}, device_id_type=MESH)

    def red_lat_make(rnd, j, out):
        place = li if out else lax.rem(li - j + n_lat, n_lat)
        return pltpu.make_async_remote_copy(
            src_ref=red_lat.at[rnd, li], dst_ref=red_lat.at[rnd, place],
            send_sem=lat_send.at[rnd, j], recv_sem=lat_recv.at[rnd, j],
            device_id={"lat": lax.rem(li + j, n_lat), "lon": lo}, device_id_type=MESH)

    sums_row = lax.broadcasted_iota(jnp.int32, (8, clon), 0)

    def reduce_start(rnd, values):
        tile = jnp.zeros((8, clon), F32)
        for n, value in enumerate(values):
            tile = jnp.where(sums_row == n, value, tile)
        red_lon[rnd, lo] = tile
        for j in range(1, n_lon):
            red_lon_make(rnd, j, True).start()

    def reduce_turn(rnd):
        for j in range(1, n_lon):
            red_lon_make(rnd, j, False).wait_recv()
        red_lat[rnd, li] = jnp.sum(red_lon[rnd], axis=0)

        @pl.loop(1, n_lat)
        def _(j):
            red_lat_make(rnd, j, True).start()

    def reduce_end(rnd):
        @pl.loop(1, n_lat)
        def _(j):
            red_lat_make(rnd, j, False).wait_recv()
        return jnp.sum(red_lat[rnd], axis=0)

    def total(x):
        return jnp.sum(jnp.sum(x, axis=0, keepdims=True), axis=1, keepdims=True)

    def squares(x):
        return total(jnp.sum((x * x).reshape(-1, 8, clon), axis=0))

    def column_total(cols):
        return jnp.sum(sum(cols), axis=0, keepdims=True)

    recv_wide(term_make(0))
    apply_model(0, True)
    send_fetch(0)
    send_parts(0)
    bb_part = squares(parts_t[0])
    p1 = observe(0)
    u1 = [w_col[b] * p1[b] for b in range(cap)]
    spread(1, u1)
    reduce_start(0, [bb_part, column_total([u1[b] * p1[b] for b in range(cap)])])
    reduce_turn(0)
    recv_wide(term_make(1))
    apply_model(1, True)
    send_fetch(1)
    send_parts(1)
    sums = reduce_end(0)
    bb, s1 = sums[0:1, 0:1], sums[1:2, 0:1]
    alpha1 = bb / (bb + s1)
    left1 = s1 / (bb + s1)
    rr_part = squares(left1 * parts_t[0] - alpha1 * parts_t[1])
    g1 = observe(1)
    pr = [left1 * p1[b] - alpha1 * g1[b] for b in range(cap)]
    ur = [w_col[b] * pr[b] for b in range(cap)]
    spread(2, ur)
    reduce_start(1, [rr_part, column_total([ur[b] * pr[b] for b in range(cap)]),
                     column_total([ur[b] * p1[b] for b in range(cap)])])
    reduce_turn(1)
    recv_wide(term_make(2))
    apply_model(2, False)
    send_parts(2)
    sums = reduce_end(1)
    rr, srr, sr1 = sums[0:1, 0:1], sums[1:2, 0:1], sums[2:3, 0:1]
    beta = rr / bb
    curve = rr + beta * beta * bb + (srr + 2.0 * beta * sr1 + beta * beta * s1)
    alpha2 = rr / curve
    for rnd in range(3):
        for j in range(1, n_lon):
            part_make(rnd, j, False).wait_recv()

    @pl.loop(0, levels)
    def _(k):
        b0, t1, tr = parts_o[0, k], parts_o[1, k], parts_o[2, k]
        r1 = left1 * b0 - alpha1 * t1
        inc_out[k] = alpha1 * b0 + alpha2 * (r1 + beta * b0)
        res_out[k] = r1 - alpha2 * (r1 + tr + beta * (b0 + t1))

    done_wide(rate_make)
    done_wide(code_make)
    for rnd in range(3):
        done_wide(term_make(rnd))
        for j in range(1, n_lon):
            part_make(rnd, j, True).wait_send()
    for rnd in range(2):
        for j in range(1, n_lon):
            fetch_make(rnd, j, True).wait_send()
            red_lon_make(rnd, j, True).wait_send()

        @pl.loop(1, n_lat)
        def _(j, rnd=rnd):
            red_lat_make(rnd, j, True).wait_send()


def shards(n_lat, n_lon, courant, obs_matrix, obs_weight, innovation, block_owner, block_row, block_count):
    _, levels, clat, clon = courant.shape
    cap = block_row.shape[1]
    share = levels // n_lon
    ext = clat + 2 * HALO
    tile_rows = n_lon * ext
    unit = clon // cap
    src_pad = -(-3 * n_lon // unit) * unit
    vmem = pl.BlockSpec(memory_space=pltpu.VMEM)
    smem = pl.BlockSpec(memory_space=pltpu.SMEM)
    hbm = pl.BlockSpec(memory_space=pl.ANY)
    dma = pltpu.SemaphoreType.DMA
    out = jax.ShapeDtypeStruct((levels, clat, clon), F32)
    return pl.pallas_call(
        functools.partial(kernel, n_lat, n_lon),
        out_shape=(out, out),
        in_specs=[hbm, hbm, vmem, vmem, smem, smem, smem],
        out_specs=(vmem, vmem),
        scratch_shapes=[
            pltpu.VMEM((2, share, n_lon, ext, clon), F32),
            pltpu.VMEM((5, share, tile_rows, clon), F32),
            pltpu.VMEM((cap, clon, clon), F32),
            pltpu.VMEM((3, src_pad, cap, clon), F32),
            pltpu.VMEM((src_pad, cap, clon), F32),
            pltpu.VMEM((3, cap, clon), F32),
            pltpu.VMEM((share * tile_rows, src_pad * cap), BF16),
            pltpu.VMEM((n_lon * cap, share * tile_rows), BF16),
            pltpu.VMEM((share, tile_rows, clon), F32),
            pltpu.VMEM((share, tile_rows, clon), F32),
            pltpu.VMEM((3, n_lon, share, clat, clon), F32),
            pltpu.VMEM((3, levels, clat, clon), F32),
            pltpu.VMEM((2, n_lon, cap, clon), F32),
            pltpu.VMEM((2, n_lon, cap, clon), F32),
            pltpu.VMEM((2, n_lon, 8, clon), F32),
            pltpu.VMEM((2, n_lat, 8, clon), F32),
            dma, dma,
            dma((5, 3, n_lon)), dma((5, 3, n_lon)),
            dma((2, n_lon)), dma((2, n_lon)),
            dma((3, n_lon)), dma((3, n_lon)),
            dma((2, n_lon)), dma((2, n_lon)),
            dma((2, n_lat)), dma((2, n_lat)),
        ],
        compiler_params=pltpu.CompilerParams(collective_id=0, has_side_effects=True),
    )(courant, obs_matrix, obs_weight, innovation, block_owner, block_row, block_count)


def solution(mesh):
    placed = (
        P(None, None, "lat", "lon"),
        P("lat", "lon", None, None),
        P("lat", "lon", None),
        P("lat", "lon", None),
        P("lat", "lon", None),
        P("lat", "lon"),
        P("lat", "lon"),
    )
    return jax.shard_map(
        functools.partial(shards, mesh.shape["lat"], mesh.shape["lon"]),
        mesh=mesh,
        in_specs=placed,
        out_specs=(P(None, "lat", "lon"), P(None, "lat", "lon")),
        check_vma=False,
    )
```

time: 284 us -> 48.6 us (0.17)
  blocking collectives: 140 us -> 0 us
  starting transfers between devices: 50.7 us -> 0 us
  Pallas kernels: 0 us -> 44.1 us
  waiting for transfers between devices: 41.9 us -> 0 us
  other arithmetic: 28.9 us -> 0 us
  local copies, waits for them, and re-layouts: 11.5 us -> 2.94 us
  between operations: 5.88 us -> 1.32 us
  matrix products: 3.45 us -> 0 us
    psum x3 -> x0, blocking collectives: 120 us -> none  [the longest x2 81.3 us: squares(): return lax.psum(jnp.sum(vector * vector), ('lat', 'lon'))]
    pallas_call x0 -> x1, Pallas kernels: none -> 44.1 us  [shards(): pl.pallas_call(functools.partial(kernel, n_lat, n_lon), out_shape=(out, o...]
    ppermute x24 -> x0, starting transfers between devices: 40.9 us -> none  [the longest x12 35.1 us: padded_2(): lax.ppermute(head, axis, [((i + 1) % count, i) for i in range(count)])]
    ppermute x24 -> x0, waiting for transfers between devices: 33.8 us -> none  [the longest x12 31.9 us: padded_2(): lax.ppermute(tail, axis, [(i, (i + 1) % count) for i in range(count)])]
    all_to_all x3 -> x0, blocking collectives: 19.8 us -> none  [the longest x2 12.3 us: to_owner(): lax.all_to_all(outgoing, 'lon', split_axis=0, concat_axis=0, tiled=True)]
    mul x26 -> x0, other arithmetic: 19 us -> none  [the longest x10 9.2 us: model_adjoint(): padded = fresh_field * edge_mask(margin)]
    all_to_all x3 -> x0, starting transfers between devices: 9.72 us -> none  [the longest x1 3.25 us: to_owner(): lax.all_to_all(outgoing, 'lon', split_axis=0, concat_axis=0, tiled=True)]
    all_to_all x3 -> x0, waiting for transfers between devices: 8.16 us -> none  [the longest x1 3.73 us: shards(): lax.all_to_all(state_rows[asked_rows], 'lon', split_axis=0, concat_axis=0...]
  transfers between devices with their start and end apart: 27 -> 0, of which waited for: 15 -> 0; matrix products, arithmetic and copies ran while one was open for 3% -> 0% of each run, Pallas kernels for 0% -> 0%
where the time goes in v1:
time: 48.6 us; the launch traced here: 48.4 us
  Pallas kernels  44.1 us (91%)
  local copies, waits for them, and re-layouts  2.94 us (6%)
  between operations  1.32 us (3%)
    pallas_call x1, Pallas kernels, shards(): pl.pallas_call(functools.partial(kernel, n_lat, n_lon), out_shape=(out, o...  44.1 us
    unnamed x7, local copies, waits for them, and re-layouts  2.94 us

profile of v1, /device:TPU:0, one launch (start us, length us, event | category | flops | bytes accessed | tf_op | source)
XLA Modules:
  0.0 48.4 jit_solution(170318526524033532)
XLA Ops:
  0.6 0.0 copy-start.1
  1.3 0.0 copy-done.1
  1.3 0.7 %copy.9.owner = s32[1,8,1]{2,1,0:T(8,128)} copy(s32[1,8,1]{1,2,0:T(1,128)S(1)} %copy-done.1) | data formatting | bytes 64 | tf_op args[4]
  2.0 44.1 %shard_map.86 = (f32[16,16,128]{2,1,0:T(8,128)}, f32[16,16,128]{2,1,0:T(8,128)}) custom-call(f32[2,16,16,128]{3,2,1,0:T(8,128)} %courant.1, f32[1,8,128,128]{3,2,1,0:T(8,128)} %obs.1, f32[1,8,128]{2,1,0:T(8,128)} %weight.1, f32[1,8,128]{2,1,0:T(8,128)} %innov.1, s32[1,8,1]{2,1,0:T(8,128)} %copy.9.owner, s32[1,8]{1,0:T(1,128)} %row.1, s32[1,1]{1,0:T(1,128)S(6)} %copy.12.count), custom_call_target="tpu_custom_call" | custom-call | tf_op jit(solution)/shard_map/pallas_call | solution.py:419
  46.1 0.0 copy-start
  46.1 1.6 %copy.13 = f32[16,16,128]{2,1,0:T(8,128)} copy(f32[16,16,128]{2,1,0:T(8,128)} %get-tuple-element.4) | data formatting | bytes 262144
  47.8 0.0 copy-done
  47.8 0.7 %copy.14 = f32[16,16,128]{2,1,0:T(8,128)} copy(f32[16,16,128]{2,1,0:T(8,128)S(1)} %copy-done) | data formatting | bytes 262144
Async XLA Ops:
  0.6 0.7 %copy-start.1 = (s32[1,8,1]{1,2,0:T(1,128)S(1)}, s32[1,8,1]{1,2,0:T(1,128)}, u32[]{:S(2)}) copy-start(s32[1,8,1]{1,2,0:T(1,128)} %param.11) | copy-start | bytes 100
  46.1 1.6 %copy-start = (f32[16,16,128]{2,1,0:T(8,128)S(1)}, f32[16,16,128]{2,1,0:T(8,128)}, u32[]{:S(2)}) copy-start(f32[16,16,128]{2,1,0:T(8,128)} %get-tuple-element.5) | copy-start | bytes 393220

commit v2 on v1

--- a/solution.py
+++ b/solution.py
@@ -33,21 +33,23 @@
 def kernel(
     n_lat, n_lon,
     courant, obs, weight, innov, owner, row, count,
-    inc_out, res_out,
-    rate_in, rates, obs_v, terms, codes, code_out, spread_mat, gather_mat,
-    field, moved, parts_t, parts_o, fetch_out, fetch_in, red_lon, red_lat,
-    obs_sem, own_sem, wide_send, wide_recv, fetch_send, fetch_recv, part_send, part_recv,
+    parts_o, coef_out,
+    flow, rate_in, rates, obs_v, terms, codes, code_out, spread_mat, gather_mat,
+    field, moved, parts_t, fetch_out, fetch_in, red_lon, red_lat,
+    obs_sem, own_sem, flow_sem, wide_send, wide_recv, fetch_send, fetch_recv, part_send, part_recv,
     lon_send, lon_recv, lat_send, lat_recv,
 ):
     li = lax.axis_index("lat")
     lo = lax.axis_index("lon")
-    levels, clat, clon = inc_out.shape
+    _, levels, clat, clon = parts_o.shape
     cap = obs_v.shape[0]
     share = levels // n_lon
     ext = clat + 2 * HALO
     tile_rows = n_lon * ext
     n_src = 3 * n_lon
 
+    flow_copy = pltpu.make_async_copy(courant, flow, flow_sem)
+    flow_copy.start()
     obs_copy = pltpu.make_async_copy(obs.at[0], obs_v, obs_sem)
     obs_copy.start()
 
@@ -60,8 +62,6 @@
         else:
             pl.when(exists(d))(run)
 
-    pairs = [(d, j) for d in (-1, 1, 0) for j in range(n_lon) if (d, j) != (0, 0)]
-
     def lon_at(j):
         return lax.rem(lo + j + n_lon, n_lon)
 
@@ -69,6 +69,10 @@
 
     def greet(lat, lon):
         pl.semaphore_signal(barrier, inc=1, device_id={"lat": lat, "lon": lon}, device_id_type=MESH)
+
+    @pl.loop(1, n_lat)
+    def _(j):
+        greet(lax.rem(li + j, n_lat), lo)
 
     for d in (-1, 1):
         def hello(d=d):
@@ -78,17 +82,13 @@
     for j in range(1, n_lon):
         greet(li, lon_at(j))
 
-    @pl.loop(1, n_lat)
-    def _(j):
-        greet(lax.rem(li + j, n_lat), lo)
-
     sub = lax.broadcasted_iota(jnp.int32, (cap, clon), 0)
     live = count[0, 0]
     scal = []
     for b in range(cap):
         r = row[0, b]
         lev = lax.div(r, jnp.int32(clat))
-        scal.append((r - lev * clat, (lev * n_lon + owner[0, b, 0]) * ext))
+        scal.append((r - lev * clat, (lev * n_lon + owner[0, b]) * ext))
     for d in (-1, 0, 1):
         tile = jnp.full((cap, clon), -1, jnp.int32)
         for b in range(cap):
@@ -124,7 +124,7 @@
             src, dst = pl.ds(clat - HALO, HALO), pl.ds(0, HALO)
         else:
             src, dst = pl.ds(0, HALO), pl.ds(HALO + clat, HALO)
-        return wide(1, d, j, courant.at[:, levs, src, :], rate_in.at[:, :, tile, dst, :])
+        return wide(1, d, j, flow.at[:, levs, src, :], rate_in.at[:, :, tile, dst, :])
 
     def term_copy(rnd, d, j, slot):
         return wide(2 + rnd, d, j, terms.at[rnd, n_lon + lo], terms.at[rnd, slot])
@@ -163,8 +163,9 @@
         return lambda d, j, out: term_copy(rnd, d, j, send_slot(d) if out else recv_slot(d, j))
 
     own_rate = pltpu.make_async_copy(
-        courant.at[:, pl.ds(lo * share, share), :, :],
+        flow.at[:, pl.ds(lo * share, share), :, :],
         rate_in.at[:, :, lo, pl.ds(HALO, clat), :], own_sem)
+    flow_copy.wait()
     start_wide(rate_make)
     start_wide(code_make)
     own_rate.start()
@@ -247,7 +248,7 @@
         flat = dot3(spread_mat[...], terms[rnd].reshape(n_blocks, clon))
         field[...] = flat.reshape(share, tile_rows, clon)
 
-        @pl.loop(0, share)
+        @pl.loop(0, share, unroll=share)
         def _(k):
             y = field[k]
             for _ in range(STEPS):
@@ -380,12 +381,11 @@
         for j in range(1, n_lon):
             part_make(rnd, j, False).wait_recv()
 
-    @pl.loop(0, levels)
-    def _(k):
-        b0, t1, tr = parts_o[0, k], parts_o[1, k], parts_o[2, k]
-        r1 = left1 * b0 - alpha1 * t1
-        inc_out[k] = alpha1 * b0 + alpha2 * (r1 + beta * b0)
-        res_out[k] = r1 - alpha2 * (r1 + tr + beta * (b0 + t1))
+    coef_row = sums_row
+    tile = jnp.zeros((8, clon), F32)
+    for n, value in enumerate((alpha1, left1, alpha2, beta)):
+        tile = jnp.where(coef_row == n, value, tile)
+    coef_out[...] = tile
 
     done_wide(rate_make)
     done_wide(code_make)
@@ -415,13 +415,16 @@
     smem = pl.BlockSpec(memory_space=pltpu.SMEM)
     hbm = pl.BlockSpec(memory_space=pl.ANY)
     dma = pltpu.SemaphoreType.DMA
-    out = jax.ShapeDtypeStruct((levels, clat, clon), F32)
-    return pl.pallas_call(
+    parts, coef = pl.pallas_call(
         functools.partial(kernel, n_lat, n_lon),
-        out_shape=(out, out),
+        out_shape=(
+            jax.ShapeDtypeStruct((3, levels, clat, clon), F32),
+            jax.ShapeDtypeStruct((8, clon), F32),
+        ),
         in_specs=[hbm, hbm, vmem, vmem, smem, smem, smem],
         out_specs=(vmem, vmem),
         scratch_shapes=[
+            pltpu.VMEM((2, levels, clat, clon), F32),
             pltpu.VMEM((2, share, n_lon, ext, clon), F32),
             pltpu.VMEM((5, share, tile_rows, clon), F32),
             pltpu.VMEM((cap, clon, clon), F32),
@@ -433,12 +436,11 @@
             pltpu.VMEM((share, tile_rows, clon), F32),
             pltpu.VMEM((share, tile_rows, clon), F32),
             pltpu.VMEM((3, n_lon, share, clat, clon), F32),
-            pltpu.VMEM((3, levels, clat, clon), F32),
             pltpu.VMEM((2, n_lon, cap, clon), F32),
             pltpu.VMEM((2, n_lon, cap, clon), F32),
             pltpu.VMEM((2, n_lon, 8, clon), F32),
             pltpu.VMEM((2, n_lat, 8, clon), F32),
-            dma, dma,
+            dma, dma, dma,
             dma((5, 3, n_lon)), dma((5, 3, n_lon)),
             dma((2, n_lon)), dma((2, n_lon)),
             dma((3, n_lon)), dma((3, n_lon)),
@@ -446,7 +448,13 @@
             dma((2, n_lat)), dma((2, n_lat)),
         ],
         compiler_params=pltpu.CompilerParams(collective_id=0, has_side_effects=True),
-    )(courant, obs_matrix, obs_weight, innovation, block_owner, block_row, block_count)
+    )(courant, obs_matrix, obs_weight, innovation, block_owner[:, :, 0], block_row, block_count)
+    alpha1, left1, alpha2, beta = (coef[n][None, None, :] for n in range(4))
+    b0, t1, tr = parts[0], parts[1], parts[2]
+    r1 = left1 * b0 - alpha1 * t1
+    increment = alpha1 * b0 + alpha2 * (r1 + beta * b0)
+    residual = r1 - alpha2 * (r1 + tr + beta * (b0 + t1))
+    return increment, residual
 
 
 def solution(mesh):

time: 48.6 us -> 43.1 us (0.89)
  Pallas kernels: 44.1 us -> 38.9 us
  local copies, waits for them, and re-layouts: 2.94 us -> 0.84 us
  other arithmetic: 0 us -> 1.79 us
    pallas_call x1, Pallas kernels: 44.1 us -> 38.9 us  [shards(): pl.pallas_call(functools.partial(kernel, n_lat, n_lon), out_shape=(jax.Sh...]
    unnamed x7 -> x0, local copies, waits for them, and re-layouts: 2.94 us -> none
    sub x0 -> x1, other arithmetic: none -> 1.79 us  [shards(): residual = r1 - alpha2 * (r1 + tr + beta * (b0 + t1))]
    mul x0 -> x1, local copies, waits for them, and re-layouts: none -> 0.84 us  [shards(): increment = alpha1 * b0 + alpha2 * (r1 + beta * b0)]
where the time goes in v2:
time: 43.1 us; the launch traced here: 42.8 us
  Pallas kernels  38.9 us (90%)
  other arithmetic  1.79 us (4%)
  between operations  1.29 us (3%)
  local copies, waits for them, and re-layouts  0.84 us (2%)
    pallas_call x1, Pallas kernels, shards(): pl.pallas_call(functools.partial(kernel, n_lat, n_lon), out_shape=(jax.Sh...  38.9 us
    sub x1, other arithmetic, shards(): residual = r1 - alpha2 * (r1 + tr + beta * (b0 + t1))  1.79 us

profile of v2, /device:TPU:0, one launch (start us, length us, event | category | flops | bytes accessed | tf_op | source)
XLA Modules:
  0.0 42.8 jit_solution(1438856530906523378)
XLA Ops:
  1.3 38.9 %shard_map.86 = (f32[3,16,16,128]{3,2,1,0:T(8,128)}, f32[8,128]{1,0:T(8,128)}) custom-call(f32[2,16,16,128]{3,2,1,0:T(8,128)} %courant.1, f32[1,8,128,128]{3,2,1,0:T(8,128)} %obs.1, f32[1,8,128]{2,1,0:T(8,128)} %weight.1, f32[1,8,128]{2,1,0:T(8,128)} %innov.1, s32[1,8]{1,0:T(1,128)} %bitcast.53, s32[1,8]{1,0:T(1,128)} %row.1, s32[1,1]{1,0:T(1,128)S(6)} %copy.9.count), custom_call_target="tpu_custom_call" | custom-call | tf_op jit(solution)/shard_map/pallas_call | solution.py:418
  40.2 0.8 %slice_bitcast_fusion.3 = (f32[128]{0:T(128)S(1)}, f32[128]{0:T(128)S(1)}, f32[128]{0:T(128)S(1)}, f32[128]{0:T(128)S(1)}) fusion(f32[8,128]{1,0:T(8,128)} %get-tuple-element.4), kind=kLoop, calls=%fused_computation.17 | loop fusion | bytes 4096 | tf_op jit(solution)/shard_map/mul | solution.py:455
  41.0 1.8 %fusion.2 = (f32[16,16,128]{2,1,0:T(8,128)}, f32[16,16,128]{2,1,0:T(8,128)}) fusion(f32[3,16,16,128]{3,2,1,0:T(8,128)} %get-tuple-element.5, f32[128]{0:T(128)S(1)} %get-tuple-element.9, f32[128]{0:T(128)S(1)} %get-tuple-element.10, f32[128]{0:T(128)S(1)} %get-tuple-element.11, f32[128]{0:T(128)S(1)} %get-tuple-element.8), kind=kLoop, calls=%fused_computation.3 | loop fusion | flops 458752 | bytes 657408 | tf_op jit(solution)/shard_map/sub | solution.py:456

commit v3 on v2

--- a/solution.py
+++ b/solution.py
@@ -32,12 +32,14 @@
 
 def kernel(
     n_lat, n_lon,
-    courant, obs, weight, innov, owner, row, count,
-    parts_o, coef_out,
-    flow, rate_in, rates, obs_v, terms, codes, code_out, spread_mat, gather_mat,
+    courant, obs, weight_in, innov_in, owner_in, row_in, count_in,
+    parts_o, alpha1_out, left1_out, alpha2_out, beta_out,
+    flow, rate_in,
+    rates, obs_v, terms, codes, code_out, spread_mat, gather_mat,
     field, moved, parts_t, fetch_out, fetch_in, red_lon, red_lat,
     obs_sem, own_sem, flow_sem, wide_send, wide_recv, fetch_send, fetch_recv, part_send, part_recv,
     lon_send, lon_recv, lat_send, lat_recv,
+    weight, innov, owner, row, count, input_sems,
 ):
     li = lax.axis_index("lat")
     lo = lax.axis_index("lon")
@@ -50,6 +52,13 @@
 
     flow_copy = pltpu.make_async_copy(courant, flow, flow_sem)
     flow_copy.start()
+    small = [
+        pltpu.make_async_copy(src, dst, input_sems.at[n])
+        for n, (src, dst) in enumerate((
+            (owner_in, owner), (row_in, row), (count_in, count), (weight_in, weight), (innov_in, innov)))
+    ]
+    for copy in small:
+        copy.start()
     obs_copy = pltpu.make_async_copy(obs.at[0], obs_v, obs_sem)
     obs_copy.start()
 
@@ -81,6 +90,9 @@
         guarded(d, hello)
     for j in range(1, n_lon):
         greet(li, lon_at(j))
+
+    for copy in small:
+        copy.wait()
 
     sub = lax.broadcasted_iota(jnp.int32, (cap, clon), 0)
     live = count[0, 0]
@@ -381,11 +393,8 @@
         for j in range(1, n_lon):
             part_make(rnd, j, False).wait_recv()
 
-    coef_row = sums_row
-    tile = jnp.zeros((8, clon), F32)
-    for n, value in enumerate((alpha1, left1, alpha2, beta)):
-        tile = jnp.where(coef_row == n, value, tile)
-    coef_out[...] = tile
+    for ref, value in ((alpha1_out, alpha1), (left1_out, left1), (alpha2_out, alpha2), (beta_out, beta)):
+        ref[...] = jnp.broadcast_to(value, (1, clon)).reshape(1, 1, clon)
 
     done_wide(rate_make)
     done_wide(code_make)
@@ -412,17 +421,17 @@
     unit = clon // cap
     src_pad = -(-3 * n_lon // unit) * unit
     vmem = pl.BlockSpec(memory_space=pltpu.VMEM)
-    smem = pl.BlockSpec(memory_space=pltpu.SMEM)
     hbm = pl.BlockSpec(memory_space=pl.ANY)
     dma = pltpu.SemaphoreType.DMA
-    parts, coef = pl.pallas_call(
+    scalar = jax.ShapeDtypeStruct((1, 1, clon), F32)
+    parts, alpha1, left1, alpha2, beta = pl.pallas_call(
         functools.partial(kernel, n_lat, n_lon),
         out_shape=(
             jax.ShapeDtypeStruct((3, levels, clat, clon), F32),
-            jax.ShapeDtypeStruct((8, clon), F32),
+            scalar, scalar, scalar, scalar,
         ),
-        in_specs=[hbm, hbm, vmem, vmem, smem, smem, smem],
-        out_specs=(vmem, vmem),
+        in_specs=[hbm] * 7,
+        out_specs=(vmem,) * 5,
         scratch_shapes=[
             pltpu.VMEM((2, levels, clat, clon), F32),
             pltpu.VMEM((2, share, n_lon, ext, clon), F32),
@@ -446,10 +455,13 @@
             dma((3, n_lon)), dma((3, n_lon)),
             dma((2, n_lon)), dma((2, n_lon)),
             dma((2, n_lat)), dma((2, n_lat)),
+            pltpu.VMEM((1, cap, clon), F32), pltpu.VMEM((1, cap, clon), F32),
+            pltpu.SMEM((1, cap), jnp.int32), pltpu.SMEM((1, cap), jnp.int32),
+            pltpu.SMEM((1, 1), jnp.int32),
+            dma((5,)),
         ],
         compiler_params=pltpu.CompilerParams(collective_id=0, has_side_effects=True),
     )(courant, obs_matrix, obs_weight, innovation, block_owner[:, :, 0], block_row, block_count)
-    alpha1, left1, alpha2, beta = (coef[n][None, None, :] for n in range(4))
     b0, t1, tr = parts[0], parts[1], parts[2]
     r1 = left1 * b0 - alpha1 * t1
     increment = alpha1 * b0 + alpha2 * (r1 + beta * b0)

time: 43.1 us -> 42.1 us (0.977)
  Pallas kernels: 38.9 us -> 38.2 us
    mul x1 -> x0, local copies, waits for them, and re-layouts: 0.84 us -> none  [shards(): increment = alpha1 * b0 + alpha2 * (r1 + beta * b0)]
    pallas_call x1, Pallas kernels: 38.9 us -> 38.2 us  [shards(): pl.pallas_call(functools.partial(kernel, n_lat, n_lon), out_shape=(jax.Sh...]
    unnamed x0 -> x8, local copies, waits for them, and re-layouts: none -> 0.68 us
where the time goes in v3:
time: 42.1 us; the launch traced here: 41.9 us
  Pallas kernels  38.2 us (91%)
  other arithmetic  1.79 us (4%)
  between operations  1.32 us (3%)
  local copies, waits for them, and re-layouts  0.68 us (2%)
    pallas_call x1, Pallas kernels, shards(): pl.pallas_call(functools.partial(kernel, n_lat, n_lon), out_shape=(jax.Sh...  38.2 us
    sub x1, other arithmetic, shards(): residual = r1 - alpha2 * (r1 + tr + beta * (b0 + t1))  1.79 us

profile of v3, /device:TPU:0, one launch (start us, length us, event | category | flops | bytes accessed | tf_op | source)
XLA Modules:
  0.0 41.9 jit_solution(5525777113606704120)
XLA Ops:
  1.3 38.2 %shard_map.86 = (f32[3,16,16,128]{3,2,1,0:T(8,128)}, f32[1,1,128]{2,1,0:T(1,128)}, f32[1,1,128]{2,1,0:T(1,128)}, f32[1,1,128]{2,1,0:T(1,128)}, f32[1,1,128]{2,1,0:T(1,128)}) custom-call(f32[2,16,16,128]{3,2,1,0:T(8,128)} %courant.1, f32[1,8,128,128]{3,2,1,0:T(8,128)} %obs.1, f32[1,8,128]{2,1,0:T(8,128)} %weight_in.1, f32[1,8,128]{2,1,0:T(8,128)} %innov_in.1, ...), custom_call_target="tpu_custom_call" | custom-call | tf_op jit(solution)/shard_map/pallas_call | solution.py:427
  39.4 0.0 copy-start.3
  39.4 0.0 copy-start
  39.5 0.0 copy-start.1
  39.5 0.0 copy-start.2
  39.5 0.6 %copy-done.3 = f32[1,1,128]{2,1,0:T(1,128)S(1)} copy-done((f32[1,1,128]{2,1,0:T(1,128)S(1)}, f32[1,1,128]{2,1,0:T(1,128)}, u32[]{:S(2)}) %copy-start.3) | copy-done | bytes 536
  40.0 0.0 copy-done
  40.1 0.0 copy-done.1
  40.1 0.1 copy-done.2
  40.2 1.8 %fusion.2 = (f32[16,16,128]{2,1,0:T(8,128)}, f32[16,16,128]{2,1,0:T(8,128)}) fusion(f32[3,16,16,128]{3,2,1,0:T(8,128)} %get-tuple-element.8, f32[128]{0:T(128)S(1)} %bitcast.52, f32[128]{0:T(128)S(1)} %bitcast.50, f32[128]{0:T(128)S(1)} %bitcast.51, f32[128]{0:T(128)S(1)} %bitcast.49), kind=kLoop, calls=%fused_computation.3 | loop fusion | flops 458752 | bytes 657408 | tf_op jit(solution)/shard_map/sub | solution.py:468
Async XLA Ops:
  39.4 0.6 %copy-start.3 = (f32[1,1,128]{2,1,0:T(1,128)S(1)}, f32[1,1,128]{2,1,0:T(1,128)}, u32[]{:S(2)}) copy-start(f32[1,1,128]{2,1,0:T(1,128)} %get-tuple-element.11) | copy-start | bytes 1540
  39.4 0.6 %copy-start = (f32[1,1,128]{2,1,0:T(1,128)S(1)}, f32[1,1,128]{2,1,0:T(1,128)}, u32[]{:S(2)}) copy-start(f32[1,1,128]{2,1,0:T(1,128)} %get-tuple-element.7) | copy-start | bytes 1540
  39.5 0.6 %copy-start.1 = (f32[1,1,128]{2,1,0:T(1,128)S(1)}, f32[1,1,128]{2,1,0:T(1,128)}, u32[]{:S(2)}) copy-start(f32[1,1,128]{2,1,0:T(1,128)} %get-tuple-element.10) | copy-start | bytes 1540
  39.5 0.7 %copy-start.2 = (f32[1,1,128]{2,1,0:T(1,128)S(1)}, f32[1,1,128]{2,1,0:T(1,128)}, u32[]{:S(2)}) copy-start(f32[1,1,128]{2,1,0:T(1,128)} %get-tuple-element.9) | copy-start | bytes 1540
